TPU v7x, 128 devices: a whole 4x4x4 slice. The times are simulated.
128 devices in a mesh: row: 8 (over y, core), col: 16 (over z, x).
Axes of the slice: x: 4, y: 4, z: 4, core: 2. Of those that a mesh axis runs over, the one named last changes fastest.
Arguments:
- strong_amp: float32 [2048, 128, 128], P(('row', 'col')), may hold values from -3 to 3
- strong_rhs: float32 [2048, 128, 128], P(('row', 'col')), may hold values from -6 to 6
- strong_left: bfloat16 [2048, 128, 128], P(('row', 'col')), may hold values from -0.5 to 0.5
- strong_right: bfloat16 [2048, 128, 128], P(('row', 'col')), may hold values from -0.5 to 0.5
- strong_energy: float32 [2048, 128], P(('row', 'col')), may hold values from 1 to 4
- strong_intersection: bfloat16 [2048, 16, 128, 128], P(('row', 'col')), may hold values from -0.375 to 0.375
- strong_nb: int32 [2048, 16], P(('row', 'col')), may hold values from 0 to 63
- strong_live: int32 [2048], P(('row', 'col')), may hold values from 1 to 16
- col_send: int32 [2048, 2], P(('row', 'col')), may hold values from 0 to 15
- row_send: int32 [1024, 2], P(('row', 'col')), may hold values from 0 to 15
- weak_amp: float32 [4096, 64, 64], P(('row', 'col')), may hold values from -3 to 3
- weak_rhs: float32 [4096, 64, 64], P(('row', 'col')), may hold values from -6 to 6
- weak_blocks: bfloat16 [4096, 64, 128], P(('row', 'col')), may hold values from -0.75 to 0.75
- weak_energy: float32 [4096, 64], P(('row', 'col')), may hold values from 1 to 4
- weak_intersection: bfloat16 [4096, 16, 64, 128], P(('row', 'col')), may hold values from -0.375 to 0.375
- weak_nb: int32 [4096, 16], P(('row', 'col')), may hold values from 0 to 63
Outputs:
- strong_next: float32 [2048, 128, 128], P(('row', 'col'))
- weak_next: float32 [4096, 64, 64], P(('row', 'col'))
Inputs may be any that keep to these rules, and one draw needn't show every extreme that they name: `col_send`: entries name local strong pairs of the sending device. `row_send`: entries name local strong pairs of the sending device. `strong_nb`: entries index the reading device's pool. `weak_nb`: entries index the reading device's pool. The first strong_live neighbours of a pair are in use.
All inputs are finite; a program needn't handle non-finite values.
Results may differ from a plain program's by a relative error of at most 0.0024.
Values may be sent and summed in bfloat16 or wider, within the bound.
A program may use at most 128 MiB of HBM per device.

v0:
```python
import jax
import jax.numpy as jnp
from jax import lax
from jax.sharding import PartitionSpec as P

UPDATES = 2


def sandwich(intersection, gathered, live_mask):
    half_way = (
        jnp.einsum(
            "snab,snbc->snac", intersection, gathered, preferred_element_type=jnp.float32
        ).astype(jnp.bfloat16)
        * live_mask
    )
    return jnp.einsum("snac,sndc->sad", half_way, intersection, preferred_element_type=jnp.float32)


def pair_terms(intersection, gathered, live_mask):
    return sandwich(intersection, gathered, live_mask)


def advance(amplitude, tiles_now, rhs, left, right, energy, coupling):
    inter = jnp.einsum("sab,sbc->sac", left, tiles_now, preferred_element_type=jnp.float32)
    inter = inter + jnp.einsum("sab,sbc->sac", tiles_now, right, preferred_element_type=jnp.float32)
    residual = rhs + inter + coupling
    return amplitude - residual / (energy[:, :, None] + energy[:, None, :])


def on_device(
    strong_amp,
    strong_rhs,
    strong_left,
    strong_right,
    strong_energy,
    strong_intersection,
    strong_nb,
    strong_live,
    col_send,
    row_send,
    weak_amp,
    weak_rhs,
    weak_blocks,
    weak_energy,
    weak_intersection,
    weak_nb,
):
    width = strong_amp.shape[1]
    live_mask = (
        jnp.arange(strong_nb.shape[1], dtype=jnp.int32)[None, :] < strong_live[:, None]
    ).astype(jnp.bfloat16)[:, :, None, None]
    weak_mask = jnp.ones((weak_nb.shape[0], weak_nb.shape[1], 1, 1), jnp.bfloat16)
    weak_width = weak_amp.shape[1]
    left_weak = weak_blocks[:, :, :weak_width]
    right_weak = weak_blocks[:, :, weak_width:]
    for update_step in range(UPDATES):
        tiles_now = strong_amp.astype(jnp.bfloat16)
        col_pool = lax.all_to_all(
            tiles_now[col_send], "col", split_axis=0, concat_axis=0, tiled=True
        )
        row_pool = lax.all_to_all(
            tiles_now[row_send], "row", split_axis=0, concat_axis=0, tiled=True
        )
        tile_pool = jnp.concatenate(
            [tiles_now, col_pool.reshape(-1, width, width), row_pool.reshape(-1, width, width)],
            axis=0,
        )
        coupling = pair_terms(strong_intersection, tile_pool[strong_nb], live_mask)
        weak_coupling = pair_terms(weak_intersection, tile_pool[weak_nb], weak_mask)
        weak_tiles = weak_amp.astype(jnp.bfloat16)
        strong_amp = advance(
            strong_amp, tiles_now, strong_rhs, strong_left, strong_right, strong_energy, coupling
        )
        weak_amp = advance(
            weak_amp, weak_tiles, weak_rhs, left_weak, right_weak, weak_energy, weak_coupling
        )
    return (strong_amp, weak_amp)


def solution(mesh):
    in_specs = (
        P(("row", "col"), None, None),
        P(("row", "col"), None, None),
        P(("row", "col"), None, None),
        P(("row", "col"), None, None),
        P(("row", "col"), None),
        P(("row", "col"), None, None, None),
        P(("row", "col"), None),
        P(("row", "col")),
        P(("row", "col"), None),
        P(("row", "col"), None),
        P(("row", "col"), None, None),
        P(("row", "col"), None, None),
        P(("row", "col"), None, None),
        P(("row", "col"), None),
        P(("row", "col"), None, None, None),
        P(("row", "col"), None),
    )
    out_specs = (P(("row", "col"), None, None), P(("row", "col"), None, None))
    return jax.shard_map(
        on_device, mesh=mesh, in_specs=in_specs, out_specs=out_specs, check_vma=False
    )
```

profile of v0, /device:TPU:1, one launch (start us, length us, event | category | flops | bytes accessed | tf_op | source)
XLA Modules:
  0.0 186.8 jit_solution(971618845088336920)
XLA Ops:
  0.6 0.0 copy-start
  0.6 0.0 copy-start.2
  0.7 1.4 convert_element_type.39
  2.1 0.7 compare_select_fusion.2
  2.8 0.1 copy.25
  2.9 0.1 reshape.56
  3.0 1.4 gather_fusion.1
  4.4 6.0 %all-to-all-start.1 = ((bf16[8,2,128,128]{3,2,1,0:T(8,128)(2,1)}), bf16[8,2,128,128]{3,2,1,0:T(8,128)(2,1)S(1)}, u32[]{:S(2)}, u32[]{:S(2)}) async-start(bf16[8,2,128,128]{3,2,1,0:T(8,128)(2,1)} %bitcast.2), calls=%async_computation.1 | async-start | bytes 1048576 | tf_op jit(solution)/shard_map/all_to_all | solution.py:61
  10.3 0.7 compare_select_fusion.3
  11.0 0.1 copy.24
  11.1 0.1 reshape.48
  11.2 1.7 gather_fusion
  12.8 6.8 %all-to-all-done.1 = bf16[8,2,128,128]{3,2,1,0:T(8,128)(2,1)S(1)} async-done(((bf16[8,2,128,128]{3,2,1,0:T(8,128)(2,1)}), bf16[8,2,128,128]{3,2,1,0:T(8,128)(2,1)S(1)}, u32[]{:S(2)}, u32[]{:S(2)}) %all-to-all-start.1) | async-done | bytes 524320 | tf_op jit(solution)/shard_map/all_to_all | solution.py:61
  19.7 0.8 copy-done.9
  20.5 7.6 %all-to-all-start = ((bf16[16,2,128,128]{3,2,1,0:T(8,128)(2,1)}), bf16[16,2,128,128]{3,2,1,0:T(8,128)(2,1)S(1)}, u32[]{:S(2)}, u32[]{:S(2)}) async-start(bf16[16,2,128,128]{3,2,1,0:T(8,128)(2,1)} %bitcast), calls=%async_computation | async-start | bytes 2097152 | tf_op jit(solution)/shard_map/all_to_all | solution.py:58
  28.1 0.7 compare_select_fusion.1
  28.8 0.1 reshape.64
  28.9 0.7 fusion.60
  29.6 2.3 %fusion.63 = f32[16,128,128]{2,1,0:T(8,128)} fusion(bf16[16,128,128]{2,1,0:T(8,128)(2,1)} %param.18, f32[16,128,128]{2,1,0:T(8,128)S(1)} %copy-done.2), kind=kOutput, calls=%fused_computation.78 | convolution fusion | flops 67371008 | bytes 2621440 | tf_op jit(solution)/shard_map/sab,sbc->sac/dot_general | solution.py:24
  31.9 11.9 %all-to-all-done = bf16[16,2,128,128]{3,2,1,0:T(8,128)(2,1)S(1)} async-done(((bf16[16,2,128,128]{3,2,1,0:T(8,128)(2,1)}), bf16[16,2,128,128]{3,2,1,0:T(8,128)(2,1)S(1)}, u32[]{:S(2)}, u32[]{:S(2)}) %all-to-all-start) | async-done | bytes 1048608 | tf_op jit(solution)/shard_map/all_to_all | solution.py:58
  43.8 1.0 copy-done.7
  44.8 1.6 pad_maximum_fusion
  46.4 8.6 %gather_fusion.2 = bf16[256,128,128]{2,1,0:T(8,128)(2,1)} fusion(bf16[64,128,128]{2,1,0:T(8,128)(2,1)S(1)} %pad_maximum_fusion, s32[1024]{0:T(1024)S(1)} %pad_clamp_fusion.1), kind=kCustom, calls=%fused_computation.2 | custom fusion | bytes 16778240 | tf_op jit(solution)/shard_map/gather | solution.py:68
  55.1 11.6 %fusion.24 = f32[16,128,128]{2,1,0:T(8,128)} fusion(bf16[16,16,128,128]{3,2,1,0:T(8,128)(2,1)} %param.21, bf16[16,16,128,128]{3,2,1,0:T(8,128)(2,1)} %bitcast.89, bf16[16,16]{1,0:T(8,128)(2,1)S(1)} %fusion.60), kind=kOutput, calls=%fused_computation.34 | convolution fusion | flops 2155872256 | bytes 17826304 | tf_op jit(solution)/shard_map/snac,sndc->sad/dot_general | solution.py:16
  66.7 3.9 %fusion.61 = (bf16[16,128,128]{2,1,0:T(8,128)(2,1)S(1)}, f32[16,128,128]{2,1,0:T(8,128)}) fusion(f32[16,128,128]{2,1,0:T(8,128)} %param.16, f32[16,128]{1,0:T(8,128)S(1)} %copy-done.11, f32[16,128,128]{2,1,0:T(8,128)} %fusion.24, f32[16,128,128]{2,1,0:T(8,128)} %param.17, f32[16,128,128]{2,1,0:T(8,128)} %fusion.63, bf16[16,128,128]{2,1,0:T(8,128)(2,1)S(1)} %copy-done), kind=kOutput, calls=%fused_computation.76 | convolution fusion | flops 69206016 | bytes 6299648 | tf_op jit(solution)/shard_map/sab,sbc->sac/dot_general | solution.py:25
  70.7 1.4 gather_fusion.4
  72.1 6.9 %all-to-all-start.3 = ((bf16[8,2,128,128]{3,2,1,0:T(8,128)(2,1)}), bf16[8,2,128,128]{3,2,1,0:T(8,128)(2,1)}, u32[]{:S(2)}, u32[]{:S(2)}) async-start(bf16[8,2,128,128]{3,2,1,0:T(8,128)(2,1)} %bitcast.92), calls=%async_computation.3 | async-start | bytes 1048576 | tf_op jit(solution)/shard_map/all_to_all | solution.py:61
  79.0 0.1 copy.28
  79.1 0.1 reshape.96
  79.2 2.6 %fusion.54 = f32[32,64,64]{2,1,0:T(8,128)} fusion(bf16[32,64,128]{2,1,0:T(8,128)(2,1)} %param.28, f32[32,64,64]{2,1,0:T(8,128)} %param.26), kind=kOutput, calls=%fused_computation.60 | convolution fusion | flops 16908288 | bytes 1572864 | tf_op jit(solution)/shard_map/sab,sbc->sac/dot_general | solution.py:24
  81.8 1.6 gather_fusion.3
  83.5 13.9 %gather_fusion.6 = bf16[512,128,128]{2,1,0:T(8,128)(2,1)} fusion(bf16[64,128,128]{2,1,0:T(8,128)(2,1)S(1)} %pad_maximum_fusion, s32[1024]{0:T(1024)S(1)} %pad_clamp_fusion), kind=kCustom, calls=%fused_computation.6 | custom fusion | bytes 33556480 | tf_op jit(solution)/shard_map/gather | solution.py:69
  97.4 4.5 %all-to-all-start.2 = ((bf16[16,2,128,128]{3,2,1,0:T(8,128)(2,1)}), bf16[16,2,128,128]{3,2,1,0:T(8,128)(2,1)}, u32[]{:S(2)}, u32[]{:S(2)}) async-start(bf16[16,2,128,128]{3,2,1,0:T(8,128)(2,1)} %bitcast.90), calls=%async_computation.2 | async-start | bytes 2097152 | tf_op jit(solution)/shard_map/all_to_all | solution.py:58
  101.9 0.0 copy-start.5
  101.9 0.0 copy-start.10
  101.9 17.4 %fusion.30 = f32[32,64,64]{2,1,0:T(8,128)S(1)} fusion(bf16[32,16,64,128]{3,2,1,0:T(8,128)(2,1)} %param.30, bf16[32,16,128,128]{3,2,1,0:T(8,128)(2,1)} %bitcast.86), kind=kOutput, calls=%fused_computation.36 | convolution fusion | flops 1614807040 | bytes 25690112 | tf_op jit(solution)/shard_map/snac,sndc->sad/dot_general | solution.py:16
  119.3 1.4 fusion.65
  120.7 2.7 %fusion.46 = f32[32,64,64]{2,1,0:T(8,128)S(1)} fusion(f32[32,64,64]{2,1,0:T(8,128)} %param.26, f32[32,64,64]{2,1,0:T(8,128)S(1)} %fusion.30, f32[32,64,64]{2,1,0:T(8,128)} %param.27, f32[32,64,64]{2,1,0:T(8,128)} %fusion.54, f32[32,64]{1,0:T(8,128)S(1)} %copy-done.10, bf16[32,64,128]{2,1,0:T(8,128)(2,1)S(1)} %copy-done.5), kind=kOutput, calls=%fused_computation.51 | convolution fusion | flops 17694720 | bytes 6324224 | tf_op jit(solution)/shard_map/sab,sbc->sac/dot_general | solution.py:25
  123.4 1.0 copy-done.3
  124.4 1.3 fusion.50
  125.7 1.6 pad_maximum_fusion.1
  127.4 8.6 %gather_fusion.5 = bf16[256,128,128]{2,1,0:T(8,128)(2,1)} fusion(bf16[64,128,128]{2,1,0:T(8,128)(2,1)S(1)} %pad_maximum_fusion.1, s32[1024]{0:T(1024)S(1)} %pad_clamp_fusion.1), kind=kCustom, calls=%fused_computation.5 | custom fusion | bytes 16778240 | tf_op jit(solution)/shard_map/gather | solution.py:68
  136.0 13.9 %gather_fusion.7 = bf16[512,128,128]{2,1,0:T(8,128)(2,1)} fusion(bf16[64,128,128]{2,1,0:T(8,128)(2,1)S(1)} %pad_maximum_fusion.1, s32[1024]{0:T(1024)S(1)} %pad_clamp_fusion), kind=kCustom, calls=%fused_computation.7 | custom fusion | bytes 33556480 | tf_op jit(solution)/shard_map/gather | solution.py:69
  149.9 11.7 %fusion.27 = f32[16,128,128]{2,1,0:T(8,128)} fusion(bf16[16,16,128,128]{3,2,1,0:T(8,128)(2,1)} %param.21, bf16[16,16,128,128]{3,2,1,0:T(8,128)(2,1)} %bitcast.88, bf16[16,16]{1,0:T(8,128)(2,1)S(1)} %fusion.60), kind=kOutput, calls=%fused_computation.35 | convolution fusion | flops 2155872256 | bytes 17826304 | tf_op jit(solution)/shard_map/snac,sndc->sad/dot_general | solution.py:16
  161.6 0.0 copy-start.1
  161.6 18.4 %fusion.33 = f32[32,64,64]{2,1,0:T(8,128)} fusion(bf16[32,16,64,128]{3,2,1,0:T(8,128)(2,1)} %param.30, bf16[32,16,128,128]{3,2,1,0:T(8,128)(2,1)} %bitcast.87), kind=kOutput, calls=%fused_computation.37 | convolution fusion | flops 1614807040 | bytes 25690112 | tf_op jit(solution)/shard_map/snac,sndc->sad/dot_general | solution.py:16
  180.0 3.3 %fusion.39 = f32[32,64,64]{2,1,0:T(8,128)} fusion(f32[32,64,64]{2,1,0:T(8,128)S(1)} %copy-done.4, f32[32,64,64]{2,1,0:T(8,128)} %fusion.33, f32[32,64,64]{2,1,0:T(8,128)} %param.27, f32[32,64,64]{2,1,0:T(8,128)} %fusion.50, f32[32,64]{1,0:T(8,128)S(1)} %copy-done.10, bf16[32,64,128]{2,1,0:T(8,128)(2,1)S(1)} %copy-done.6), kind=kOutput, calls=%fused_computation.42 | convolution fusion | flops 17694720 | bytes 4751360 | tf_op jit(solution)/shard_map/sab,sbc->sac/dot_general | solution.py:24
  183.3 3.6 %fusion.43 = f32[16,128,128]{2,1,0:T(8,128)} fusion(f32[16,128,128]{2,1,0:T(8,128)} %get-tuple-element.3, f32[16,128,128]{2,1,0:T(8,128)} %fusion.27, f32[16,128,128]{2,1,0:T(8,128)} %param.17, f32[16,128,128]{2,1,0:T(8,128)} %fusion.65, bf16[16,128,128]{2,1,0:T(8,128)(2,1)S(1)} %copy-done.8, bf16[16,128,128]{2,1,0:T(8,128)(2,1)S(1)} %get-tuple-element.2, ...), kind=kOutput, calls=%fused_computation.47 | convolution fusion | flops 68681728 | bytes 6299648 | tf_op jit(solution)/shard_map/sab,sbc->sac/dot_general | solution.py:24
  (25 shorter events, 0.1 us)
Async XLA Ops:
  0.6 66.1 %copy-start = (bf16[16,128,128]{2,1,0:T(8,128)(2,1)S(1)}, bf16[16,128,128]{2,1,0:T(8,128)(2,1)}, u32[]{:S(2)}) copy-start(bf16[16,128,128]{2,1,0:T(8,128)(2,1)} %param.19) | copy-start | bytes 1572868
  0.6 29.0 %copy-start.2 = (f32[16,128,128]{2,1,0:T(8,128)S(1)}, f32[16,128,128]{2,1,0:T(8,128)}, u32[]{:S(2)}) copy-start(f32[16,128,128]{2,1,0:T(8,128)} %param.16) | copy-start | bytes 3145732
  4.4 15.3 %all-to-all-start.1 = ((bf16[8,2,128,128]{3,2,1,0:T(8,128)(2,1)}), bf16[8,2,128,128]{3,2,1,0:T(8,128)(2,1)S(1)}, u32[]{:S(2)}, u32[]{:S(2)}) async-start(bf16[8,2,128,128]{3,2,1,0:T(8,128)(2,1)} %bitcast.2), calls=%async_computation.1 | async-start | bytes 1048576 | tf_op jit(solution)/shard_map/all_to_all | solution.py:61
  19.7 0.8 copy-start.9
  20.5 23.4 %all-to-all-start = ((bf16[16,2,128,128]{3,2,1,0:T(8,128)(2,1)}), bf16[16,2,128,128]{3,2,1,0:T(8,128)(2,1)S(1)}, u32[]{:S(2)}, u32[]{:S(2)}) async-start(bf16[16,2,128,128]{3,2,1,0:T(8,128)(2,1)} %bitcast), calls=%async_computation | async-start | bytes 2097152 | tf_op jit(solution)/shard_map/all_to_all | solution.py:58
  43.8 1.0 copy-start.7
  55.1 11.7 %copy-start.11 = (f32[16,128]{1,0:T(8,128)S(1)}, f32[16,128]{1,0:T(8,128)}, u32[]{:S(2)}) copy-start(f32[16,128]{1,0:T(8,128)} %param.20) | copy-start | bytes 24580
  66.7 12.3 %copy-start.12 = (s32[32,16]{0,1:T(8,128)S(1)}, s32[32,16]{0,1:T(8,128)}, u32[]{:S(2)}) copy-start(s32[32,16]{0,1:T(8,128)} %param.31) | copy-start | bytes 6148
  72.1 25.3 %all-to-all-start.3 = ((bf16[8,2,128,128]{3,2,1,0:T(8,128)(2,1)}), bf16[8,2,128,128]{3,2,1,0:T(8,128)(2,1)}, u32[]{:S(2)}, u32[]{:S(2)}) async-start(bf16[8,2,128,128]{3,2,1,0:T(8,128)(2,1)} %bitcast.92), calls=%async_computation.3 | async-start | bytes 1048576 | tf_op jit(solution)/shard_map/all_to_all | solution.py:61
  97.4 28.4 %all-to-all-start.2 = ((bf16[16,2,128,128]{3,2,1,0:T(8,128)(2,1)}), bf16[16,2,128,128]{3,2,1,0:T(8,128)(2,1)}, u32[]{:S(2)}, u32[]{:S(2)}) async-start(bf16[16,2,128,128]{3,2,1,0:T(8,128)(2,1)} %bitcast.90), calls=%async_computation.2 | async-start | bytes 2097152 | tf_op jit(solution)/shard_map/all_to_all | solution.py:58
  101.9 18.8 %copy-start.5 = (bf16[32,64,128]{2,1,0:T(8,128)(2,1)S(1)}, bf16[32,64,128]{2,1,0:T(8,128)(2,1)}, u32[]{:S(2)}) copy-start(bf16[32,64,128]{2,1,0:T(8,128)(2,1)} %param.28) | copy-start | bytes 1572868
  101.9 18.8 %copy-start.10 = (f32[32,64]{1,0:T(8,128)S(1)}, f32[32,64]{1,0:T(8,128)}, u32[]{:S(2)}) copy-start(f32[32,64]{1,0:T(8,128)} %param.29) | copy-start | bytes 24580
  123.4 1.0 copy-start.3
  161.6 18.4 %copy-start.4 = (f32[32,64,64]{2,1,0:T(8,128)S(1)}, f32[32,64,64]{2,1,0:T(8,128)}, u32[]{:S(2)}) copy-start(f32[32,64,64]{2,1,0:T(8,128)} %copy-done.3) | copy-start | bytes 1572868
  161.6 18.4 %copy-start.6 = (bf16[32,64,128]{2,1,0:T(8,128)(2,1)S(1)}, bf16[32,64,128]{2,1,0:T(8,128)(2,1)}, u32[]{:S(2)}) copy-start(bf16[32,64,128]{2,1,0:T(8,128)(2,1)} %param.28) | copy-start | bytes 1572868
  161.6 21.7 %copy-start.8 = (bf16[16,128,128]{2,1,0:T(8,128)(2,1)S(1)}, bf16[16,128,128]{2,1,0:T(8,128)(2,1)}, u32[]{:S(2)}) copy-start(bf16[16,128,128]{2,1,0:T(8,128)(2,1)} %param.18) | copy-start | bytes 1572868
  161.6 25.2 %copy-start.1 = (bf16[16,128,128]{2,1,0:T(8,128)(2,1)S(1)}, bf16[16,128,128]{2,1,0:T(8,128)(2,1)}, u32[]{:S(2)}) copy-start(bf16[16,128,128]{2,1,0:T(8,128)(2,1)} %param.19) | copy-start | bytes 1572868
where the time goes:
time: 188 us; the launch traced here: 187 us
  matrix products  80.2 us (43%)
  local copies, waits for them, and re-layouts  54.6 us (29%)
  starting transfers between devices  25 us (13%)
  waiting for transfers between devices  18.7 us (10%)
  other arithmetic  7.52 us (4%)
    dot_general x4, matrix products, sandwich(): jnp.einsum('snac,sndc->sad', half_way, intersection, preferred_element_ty...  59.1 us
    gather x2, local copies, waits for them, and re-layouts, on_device(): weak_coupling = pair_terms(weak_intersection, tile_pool[weak_nb], weak_mask)  27.8 us
    gather x2, local copies, waits for them, and re-layouts, on_device(): coupling = pair_terms(strong_intersection, tile_pool[strong_nb], live_mask)  17.3 us
    all_to_all x2, starting transfers between devices, on_device(): lax.all_to_all(tiles_now[row_send], 'row', split_axis=0, concat_axis=0, t...  12.9 us
    all_to_all x2, starting transfers between devices, on_device(): lax.all_to_all(tiles_now[col_send], 'col', split_axis=0, concat_axis=0, t...  12.1 us
    all_to_all x2, waiting for transfers between devices, on_device(): lax.all_to_all(tiles_now[col_send], 'col', split_axis=0, concat_axis=0, t...  11.9 us
    dot_general x4, matrix products, advance(): jnp.einsum('sab,sbc->sac', left, tiles_now, preferred_element_type=jnp.fl...  11.8 us
    dot_general x4, matrix products, advance(): jnp.einsum('sab,sbc->sac', tiles_now, right, preferred_element_type=jnp.f...  9.36 us
  transfers between devices with their start and end apart: 4, of which 2 were waited for; matrix products, arithmetic and copies ran while one was open for 25% of the time, Pallas kernels for 0%

commit v1 on v0

v1 whole, which is shorter than its diff:
```python
import jax
import jax.numpy as jnp
from jax import lax
from jax.experimental import pallas as pl
from jax.experimental.pallas import tpu as pltpu
from jax.sharding import PartitionSpec as P

F32, BF16 = jnp.float32, jnp.bfloat16
MESH = pl.DeviceIdType.MESH
COLS, ROWS, CAP = 16, 8, 2
SIDE, DEPTH, CORES = 4, 4, 2
SP, WP, NB, WIDE, SLIM = 16, 32, 16, 128, 64
POOL, BLANK = 64, 64
ROW_AT = SP + COLS * CAP

COL_STEPS = sorted(
    ((dz, dx) for dz in range(SIDE) for dx in range(SIDE) if dz or dx),
    key=lambda s: -(min(s[0], SIDE - s[0]) + min(s[1], SIDE - s[1])),
)
ROW_STEPS = sorted(
    ((dy, dk) for dy in range(DEPTH) for dk in range(CORES) if dy or dk),
    key=lambda s: -min(s[0], DEPTH - s[0]),
)


def nn(a, b):
    return lax.dot_general(a, b, (((1,), (0,)), ((), ())), preferred_element_type=F32)


def nt(a, b):
    return lax.dot_general(a, b, (((1,), (1,)), ((), ())), preferred_element_type=F32)


def coupling(overlap, pair, pool, tile_of):
    mids = [nn(overlap[pair, n], pool[tile_of(n)]).astype(BF16) for n in range(NB)]
    total = None
    for n in range(0, NB, 2):
        term = nt(
            jnp.concatenate([mids[n], mids[n + 1]], 1),
            jnp.concatenate([overlap[pair, n], overlap[pair, n + 1]], 1),
        )
        total = term if total is None else total + term
    return total


def looped(count, unroll, body):
    def step(i, carry):
        for u in range(unroll):
            body(i * unroll + u)
        return carry

    lax.fori_loop(0, count // unroll, step, 0)


def kernel(
    s_nb, s_live, c_send, r_send, w_nb,
    s_amp_h, s_rhs_h, s_left_h, s_right_h, s_en, s_over_h,
    w_amp_h, w_rhs_h, w_blk_h, w_en, w_over_h,
    s_out_h, w_out_h,
    s_over, w_over, s_amp, s_next, s_rhs, s_left, s_right,
    w_amp, w_next, w_rhs, w_blk, s_inv, w_inv, s_base, w_base,
    pool_a, pool_b, col_a, col_b, row_a, row_b,
    load_sem, out_sem, col_ss, col_rs, row_ss, row_rs,
):
    r, c = lax.axis_index("row"), lax.axis_index("col")
    z, x = c // SIDE, lax.rem(c, SIDE)
    y, k = r // CORES, lax.rem(r, CORES)

    def col_of(step):
        return lax.rem(z + step[0], SIDE) * SIDE + lax.rem(x + step[1], SIDE)

    def row_of(step):
        return lax.rem(y + step[0], DEPTH) * CORES + lax.rem(k + step[1], CORES)

    loads = [
        pltpu.make_async_copy(source, place, load_sem.at[i])
        for i, (source, place) in enumerate(
            (
                (s_amp_h, s_amp), (s_left_h, s_left), (s_right_h, s_right), (s_rhs_h, s_rhs),
                (w_amp_h, w_amp), (w_blk_h, w_blk), (w_rhs_h, w_rhs), (s_over_h, s_over), (w_over_h, w_over),
            )
        )
    ]
    for load in loads:
        load.start()

    barrier = pltpu.get_barrier_semaphore()
    for step in COL_STEPS:
        pl.semaphore_signal(barrier, inc=1, device_id=(r, col_of(step)), device_id_type=MESH)
    for step in ROW_STEPS:
        pl.semaphore_signal(barrier, inc=1, device_id=(row_of(step), c), device_id_type=MESH)

    def exchange(amp, pool, col_buf, row_buf, update, ready):
        base_col, base_row = update * COLS, update * ROWS

        def tile(wanted):
            return amp[wanted].astype(BF16)

        copies = []
        legs = []
        for i in range(max(len(COL_STEPS), len(ROW_STEPS))):
            if i < len(COL_STEPS):
                to = col_of(COL_STEPS[i])
                legs.append((to, c_send, col_buf.at[i], SP + CAP * c, (r, to), col_ss.at[base_col + i], col_rs.at[base_col + i]))
            if i < len(ROW_STEPS):
                to = row_of(ROW_STEPS[i])
                legs.append((to, r_send, row_buf.at[i], ROW_AT + CAP * r, (to, c), row_ss.at[base_row + i], row_rs.at[base_row + i]))
        for to, wanted, buf, at, device, ss, rs in legs:
            for slot in range(CAP):
                buf[slot] = tile(wanted[to, slot])
            copies.append(
                pltpu.make_async_remote_copy(buf, pool.at[pl.ds(at, CAP)], ss, rs, device_id=device, device_id_type=MESH)
            )
            if ready is None:
                copies[-1].start()
        if ready is not None:
            ready()
            for copy in copies:
                copy.start()
        for slot in range(CAP):
            pool[SP + CAP * c + slot] = tile(c_send[c, slot])
            pool[ROW_AT + CAP * r + slot] = tile(r_send[r, slot])

        def own(p):
            pool[p] = tile(p)

        looped(SP, 4, own)
        pool[BLANK] = jnp.zeros((WIDE, WIDE), BF16)
        return copies

    def strong_base(amp):
        def body(p):
            now = amp[p].astype(BF16)
            s_base[p] = s_rhs[p] + nn(s_left[p], now) + nn(now, s_right[p])

        looped(SP, 2, body)

    def weak_base(amp):
        def body(w):
            now = amp[w].astype(BF16)
            w_base[w] = w_rhs[w] + nn(w_blk[w, :, :SLIM], now) + nn(now, w_blk[w, :, SLIM:])

        looped(WP, 4, body)

    def strong_update(amp, new, pool):
        def body(p):
            total = coupling(s_over, p, pool, lambda n: jnp.where(n < s_live[p], s_nb[p, n], BLANK))
            new[p] = amp[p] - (s_base[p] + total) * s_inv[p]

        looped(SP, 2, body)

    def weak_update(amp, new, pool):
        def body(w):
            total = coupling(w_over, w, pool, lambda n: w_nb[w, n])
            new[w] = amp[w] - (w_base[w] + total) * w_inv[w]

        looped(WP, 4, body)

    loads[0].wait()
    copies = exchange(s_amp, pool_a, col_a, row_a, 0, lambda: pl.semaphore_wait(barrier, len(COL_STEPS) + len(ROW_STEPS)))

    def strong_inverse(p):
        across = jnp.broadcast_to(s_en[pl.ds(p, 1), :], (WIDE, WIDE))
        s_inv[p] = 1.0 / (across + across.T)

    def weak_inverse(w):
        across = jnp.broadcast_to(w_en[pl.ds(w, 1), :], (SLIM, SLIM))
        w_inv[w] = 1.0 / (across + across.T)

    looped(SP, 2, strong_inverse)
    looped(WP, 2, weak_inverse)
    for load in loads[1:]:
        load.wait()
    strong_base(s_amp)
    weak_base(w_amp)
    for copy in copies:
        copy.wait()

    strong_update(s_amp, s_next, pool_a)
    copies = exchange(s_next, pool_b, col_b, row_b, 1, None)
    strong_base(s_next)
    weak_update(w_amp, w_next, pool_a)
    weak_base(w_next)
    for copy in copies:
        copy.wait()

    weak_update(w_next, w_amp, pool_b)
    weak_out = pltpu.make_async_copy(w_amp, w_out_h, out_sem.at[0])
    weak_out.start()
    strong_update(s_next, s_amp, pool_b)
    strong_out = pltpu.make_async_copy(s_amp, s_out_h, out_sem.at[1])
    strong_out.start()
    weak_out.wait()
    strong_out.wait()


def on_device(
    strong_amp, strong_rhs, strong_left, strong_right, strong_energy, strong_intersection, strong_nb, strong_live,
    col_send, row_send, weak_amp, weak_rhs, weak_blocks, weak_energy, weak_intersection, weak_nb,
):
    smem, vmem = pl.BlockSpec(memory_space=pltpu.SMEM), pl.BlockSpec(memory_space=pltpu.VMEM)
    hbm = pl.BlockSpec(memory_space=pltpu.HBM)
    strong, weak = (SP, WIDE, WIDE), (WP, SLIM, SLIM)
    return pl.pallas_call(
        kernel,
        out_shape=(jax.ShapeDtypeStruct(strong, F32), jax.ShapeDtypeStruct(weak, F32)),
        in_specs=[smem] * 5 + [hbm] * 4 + [vmem, hbm] + [hbm] * 3 + [vmem, hbm],
        out_specs=(hbm, hbm),
        scratch_shapes=[
            pltpu.VMEM((SP, NB, WIDE, WIDE), BF16),
            pltpu.VMEM((WP, NB, SLIM, WIDE), BF16),
            pltpu.VMEM(strong, F32),
            pltpu.VMEM(strong, F32),
            pltpu.VMEM(strong, F32),
            pltpu.VMEM(strong, BF16),
            pltpu.VMEM(strong, BF16),
            pltpu.VMEM(weak, F32),
            pltpu.VMEM(weak, F32),
            pltpu.VMEM(weak, F32),
            pltpu.VMEM((WP, SLIM, WIDE), BF16),
            pltpu.VMEM(strong, F32),
            pltpu.VMEM(weak, F32),
            pltpu.VMEM(strong, F32),
            pltpu.VMEM(weak, F32),
            pltpu.VMEM((POOL + 1, WIDE, WIDE), BF16),
            pltpu.VMEM((POOL + 1, WIDE, WIDE), BF16),
            pltpu.VMEM((len(COL_STEPS), CAP, WIDE, WIDE), BF16),
            pltpu.VMEM((len(COL_STEPS), CAP, WIDE, WIDE), BF16),
            pltpu.VMEM((len(ROW_STEPS), CAP, WIDE, WIDE), BF16),
            pltpu.VMEM((len(ROW_STEPS), CAP, WIDE, WIDE), BF16),
            pltpu.SemaphoreType.DMA((9,)),
            pltpu.SemaphoreType.DMA((2,)),
            pltpu.SemaphoreType.DMA((2 * COLS,)),
            pltpu.SemaphoreType.DMA((2 * COLS,)),
            pltpu.SemaphoreType.DMA((2 * ROWS,)),
            pltpu.SemaphoreType.DMA((2 * ROWS,)),
        ],
        compiler_params=pltpu.CompilerParams(
            collective_id=0, has_side_effects=True, vmem_limit_bytes=56 * 2**20
        ),
        name="amplitude_updates",
    )(
        strong_nb, strong_live, col_send, row_send, weak_nb,
        strong_amp, strong_rhs, strong_left, strong_right, strong_energy, strong_intersection,
        weak_amp, weak_rhs, weak_blocks, weak_energy, weak_intersection,
    )


def solution(mesh):
    pairs = ("row", "col")
    three, two = P(pairs, None, None), P(pairs, None)
    four = P(pairs, None, None, None)
    in_specs = (
        three, three, three, three, two, four, two, P(pairs),
        two, two, three, three, three, two, four, two,
    )
    return jax.shard_map(
        on_device, mesh=mesh, in_specs=in_specs, out_specs=(three, three), check_vma=False
    )
```

time: 188 us -> 70.6 us (0.38)
  matrix products: 80.2 us -> 0 us
  Pallas kernels: 0 us -> 60.9 us
  local copies, waits for them, and re-layouts: 54.6 us -> 8.67 us
  starting transfers between devices: 25 us -> 0 us
  waiting for transfers between devices: 18.7 us -> 0 us
  other arithmetic: 7.52 us -> 0 us
    dot_general x12 -> x0, matrix products: 80.2 us -> none  [the longest x4 59.1 us: sandwich(): jnp.einsum('snac,sndc->sad', half_way, intersection, preferred_element_ty...]
    pallas_call x0 -> x1, Pallas kernels: none -> 60.9 us  [on_device(): pl.pallas_call(kernel, out_shape=(jax.ShapeDtypeStruct(strong, F32), jax....]
    gather x8 -> x0, local copies, waits for them, and re-layouts: 51.2 us -> none  [the longest x2 27.8 us: on_device(): weak_coupling = pair_terms(weak_intersection, tile_pool[weak_nb], weak_mask)]
    all_to_all x4 -> x0, starting transfers between devices: 25 us -> none  [the longest x2 12.9 us: on_device(): lax.all_to_all(tiles_now[row_send], 'row', split_axis=0, concat_axis=0, t...]
    all_to_all x4 -> x0, waiting for transfers between devices: 18.7 us -> none  [the longest x2 11.9 us: on_device(): lax.all_to_all(tiles_now[col_send], 'col', split_axis=0, concat_axis=0, t...]
    unnamed x26 -> x5, local copies, waits for them, and re-layouts: 2.81 us -> 8.67 us
    concatenate x2 -> x0, other arithmetic: 3.26 us -> none  [on_device(): jnp.concatenate([tiles_now, col_pool.reshape(-1, width, width), row_pool....]
    convert_element_type x2 -> x0, other arithmetic: 2.16 us -> none  [the longest x1 1.43 us: on_device(): tiles_now = strong_amp.astype(jnp.bfloat16)]
  transfers between devices with their start and end apart: 4 -> 0, of which waited for: 2 -> 0; matrix products, arithmetic and copies ran while one was open for 25% -> 0% of each run, Pallas kernels for 0% -> 0%
where the time goes in v1:
time: 70.6 us; the launch traced here: 70.3 us
  Pallas kernels  60.9 us (86%)
  local copies, waits for them, and re-layouts  8.67 us (12%)
    pallas_call x1, Pallas kernels, on_device(): pl.pallas_call(kernel, out_shape=(jax.ShapeDtypeStruct(strong, F32), jax....  60.9 us
    unnamed x5, local copies, waits for them, and re-layouts  8.67 us

profile of v1, /device:TPU:1, one launch (start us, length us, event | category | flops | bytes accessed | tf_op | source)
XLA Modules:
  0.0 70.3 jit_solution(959249841341520295)
XLA Ops:
  0.6 1.3 %copy.19.r_send = s32[8,2]{1,0:T(8,128)} copy(s32[8,2]{0,1:T(2,128)} %param.25) | data formatting | bytes 128 | tf_op args[9]
  2.0 1.4 %copy.18.c_send = s32[16,2]{1,0:T(8,128)} copy(s32[16,2]{0,1:T(2,128)} %param.24) | data formatting | bytes 256 | tf_op args[8]
  3.3 1.4 %copy.20.w_nb = s32[32,16]{1,0:T(8,128)} copy(s32[32,16]{0,1:T(8,128)} %param.31) | data formatting | bytes 4096 | tf_op args[15]
  4.7 60.9 %amplitude_updates.1 = (f32[16,128,128]{2,1,0:T(8,128)}, f32[32,64,64]{2,1,0:T(8,128)}) custom-call(s32[16,16]{1,0:T(8,128)} %s_nb.1, s32[16]{0:T(128)} %s_live.1, s32[16,2]{1,0:T(8,128)} %copy.18.c_send, s32[8,2]{1,0:T(8,128)} %copy.19.r_send, s32[32,16]{1,0:T(8,128)} %copy.20.w_nb, f32[16,128,128]{2,1,0:T(8,128)} %s_amp_h.1, f32[16,128,128]{2,1,0:T(8,128)} %s_rhs_h.1, ...), custom_call_target="tpu_custom_call" | custom-call | tf_op jit(solution)/shard_map/amplitude_updates/pallas_call | solution.py:204
  65.7 2.3 %copy.23 = f32[16,128,128]{2,1,0:T(8,128)} copy(f32[16,128,128]{2,1,0:T(8,128)} %get-tuple-element.4) | data formatting | bytes 2097152
  68.0 2.3 %copy.24 = f32[32,64,64]{2,1,0:T(8,128)} copy(f32[32,64,64]{2,1,0:T(8,128)} %get-tuple-element.5) | data formatting | bytes 1048576

commit v2 on v1

--- a/solution.py
+++ b/solution.py
@@ -52,15 +52,14 @@
     lax.fori_loop(0, count // unroll, step, 0)
 
 
-def kernel(
+def first_update(
     s_nb, s_live, c_send, r_send, w_nb,
     s_amp_h, s_rhs_h, s_left_h, s_right_h, s_en, s_over_h,
     w_amp_h, w_rhs_h, w_blk_h, w_en, w_over_h,
-    s_out_h, w_out_h,
-    s_over, w_over, s_amp, s_next, s_rhs, s_left, s_right,
-    w_amp, w_next, w_rhs, w_blk, s_inv, w_inv, s_base, w_base,
-    pool_a, pool_b, col_a, col_b, row_a, row_b,
-    load_sem, out_sem, col_ss, col_rs, row_ss, row_rs,
+    s_over, w_over, pool_b, s_pre, w_pre, s_inv, w_inv,
+    s_amp, s_next, s_rhs, s_left, s_right, w_amp, w_next, w_rhs, w_blk, s_base, w_base,
+    pool_a, col_a, col_b, row_a, row_b,
+    load_sem, col_ss, col_rs, row_ss, row_rs,
 ):
     r, c = lax.axis_index("row"), lax.axis_index("col")
     z, x = c // SIDE, lax.rem(c, SIDE)
@@ -107,7 +106,7 @@
                 legs.append((to, r_send, row_buf.at[i], ROW_AT + CAP * r, (to, c), row_ss.at[base_row + i], row_rs.at[base_row + i]))
         for to, wanted, buf, at, device, ss, rs in legs:
             for slot in range(CAP):
-                buf[slot] = tile(wanted[to, slot])
+                buf[slot] = tile(wanted[slot, to])
             copies.append(
                 pltpu.make_async_remote_copy(buf, pool.at[pl.ds(at, CAP)], ss, rs, device_id=device, device_id_type=MESH)
             )
@@ -118,8 +117,8 @@
             for copy in copies:
                 copy.start()
         for slot in range(CAP):
-            pool[SP + CAP * c + slot] = tile(c_send[c, slot])
-            pool[ROW_AT + CAP * r + slot] = tile(r_send[r, slot])
+            pool[SP + CAP * c + slot] = tile(c_send[slot, c])
+            pool[ROW_AT + CAP * r + slot] = tile(r_send[slot, r])
 
         def own(p):
             pool[p] = tile(p)
@@ -128,33 +127,35 @@
         pool[BLANK] = jnp.zeros((WIDE, WIDE), BF16)
         return copies
 
-    def strong_base(amp):
+    def strong_base(amp, out):
         def body(p):
             now = amp[p].astype(BF16)
-            s_base[p] = s_rhs[p] + nn(s_left[p], now) + nn(now, s_right[p])
-
-        looped(SP, 2, body)
-
-    def weak_base(amp):
+            rest = s_rhs[p] + nn(s_left[p], now) + nn(now, s_right[p])
+            out[p] = amp[p] - rest * s_inv[p]
+
+        looped(SP, 4, body)
+
+    def weak_base(amp, out):
         def body(w):
             now = amp[w].astype(BF16)
-            w_base[w] = w_rhs[w] + nn(w_blk[w, :, :SLIM], now) + nn(now, w_blk[w, :, SLIM:])
-
-        looped(WP, 4, body)
-
-    def strong_update(amp, new, pool):
+            rest = w_rhs[w] + nn(w_blk[w, :, :SLIM], now) + nn(now, w_blk[w, :, SLIM:])
+            out[w] = amp[w] - rest * w_inv[w]
+
+        looped(WP, 8, body)
+
+    def strong_update(new, pool):
         def body(p):
             total = coupling(s_over, p, pool, lambda n: jnp.where(n < s_live[p], s_nb[p, n], BLANK))
-            new[p] = amp[p] - (s_base[p] + total) * s_inv[p]
-
-        looped(SP, 2, body)
-
-    def weak_update(amp, new, pool):
+            new[p] = s_base[p] - total * s_inv[p]
+
+        looped(SP, 4, body)
+
+    def weak_update(new, pool):
         def body(w):
-            total = coupling(w_over, w, pool, lambda n: w_nb[w, n])
-            new[w] = amp[w] - (w_base[w] + total) * w_inv[w]
-
-        looped(WP, 4, body)
+            total = coupling(w_over, w, pool, lambda n: w_nb[n, w])
+            new[w] = w_base[w] - total * w_inv[w]
+
+        looped(WP, 8, body)
 
     loads[0].wait()
     copies = exchange(s_amp, pool_a, col_a, row_a, 0, lambda: pl.semaphore_wait(barrier, len(COL_STEPS) + len(ROW_STEPS)))
@@ -171,27 +172,86 @@
     looped(WP, 2, weak_inverse)
     for load in loads[1:]:
         load.wait()
-    strong_base(s_amp)
-    weak_base(w_amp)
+    strong_base(s_amp, s_base)
+    weak_base(w_amp, w_base)
     for copy in copies:
         copy.wait()
 
-    strong_update(s_amp, s_next, pool_a)
+    strong_update(s_next, pool_a)
     copies = exchange(s_next, pool_b, col_b, row_b, 1, None)
-    strong_base(s_next)
-    weak_update(w_amp, w_next, pool_a)
-    weak_base(w_next)
+    strong_base(s_next, s_pre)
+    weak_update(w_next, pool_a)
+    weak_base(w_next, w_pre)
     for copy in copies:
         copy.wait()
 
-    weak_update(w_next, w_amp, pool_b)
-    weak_out = pltpu.make_async_copy(w_amp, w_out_h, out_sem.at[0])
-    weak_out.start()
-    strong_update(s_next, s_amp, pool_b)
-    strong_out = pltpu.make_async_copy(s_amp, s_out_h, out_sem.at[1])
-    strong_out.start()
-    weak_out.wait()
-    strong_out.wait()
+
+UNIT, UNITS, WEAK_STEP = 4, 8, 8
+
+
+def second_update(
+    s_nb, s_live, w_nb, s_over, w_over, pool, s_pre, w_pre, s_inv, w_inv,
+    s_out, w_out, s_sum, s_new, w_new, s_sem, w_sem,
+):
+    def parts(p):
+        return lax.div(s_live[p] + (UNIT - 1), UNIT)
+
+    total = parts(0)
+    for p in range(1, SP):
+        total = total + parts(p)
+
+    def strong_units(state):
+        p, j = state
+        for _ in range(UNITS):
+            real = p < SP
+            at = jnp.minimum(p, SP - 1)
+            live = jnp.where(real, s_live[at], 0)
+            mids = [
+                nn(s_over[at, j + t], pool[jnp.where(j + t < live, s_nb[at, j + t], BLANK)]).astype(BF16)
+                for t in range(UNIT)
+            ]
+            term = None
+            for t in range(0, UNIT, 2):
+                more = nt(
+                    jnp.concatenate([mids[t], mids[t + 1]], 1),
+                    jnp.concatenate([s_over[at, j + t], s_over[at, j + t + 1]], 1),
+                )
+                term = more if term is None else term + more
+            s_sum[p] = jnp.where(j == 0, 0.0, s_sum[p]) + term
+            last = j + UNIT >= live
+            p = jnp.where(last & real, p + 1, p)
+            j = jnp.where(last, 0, j + UNIT)
+        return p, j
+
+    def weak_copy(i):
+        rows = pl.ds(i * WEAK_STEP, WEAK_STEP)
+        return pltpu.make_async_copy(w_new.at[rows], w_out.at[rows], w_sem.at[i])
+
+    def both(i, state):
+        for u in range(WEAK_STEP):
+            w = i * WEAK_STEP + u
+            w_new[w] = w_pre[w] - coupling(w_over, w, pool, lambda n: w_nb[n, w]) * w_inv[w]
+        state = strong_units(state)
+        weak_copy(i).start()
+        return state
+
+    steps = WP // WEAK_STEP
+    state = lax.fori_loop(0, steps, both, (jnp.int32(0), jnp.int32(0)))
+    rounds = lax.div(total + (UNITS - 1), UNITS)
+    lax.fori_loop(steps, rounds, lambda _, state: strong_units(state), state)
+
+    quarter = SP // 4
+    copies = []
+    for q in range(4):
+        for p in range(q * quarter, (q + 1) * quarter):
+            s_new[p] = s_pre[p] - s_sum[p] * s_inv[p]
+        rows = pl.ds(q * quarter, quarter)
+        copies.append(pltpu.make_async_copy(s_new.at[rows], s_out.at[rows], s_sem.at[q]))
+        copies[-1].start()
+    for i in range(steps):
+        weak_copy(i).wait()
+    for copy in copies:
+        copy.wait()
 
 
 def on_device(
@@ -201,14 +261,25 @@
     smem, vmem = pl.BlockSpec(memory_space=pltpu.SMEM), pl.BlockSpec(memory_space=pltpu.VMEM)
     hbm = pl.BlockSpec(memory_space=pltpu.HBM)
     strong, weak = (SP, WIDE, WIDE), (WP, SLIM, SLIM)
-    return pl.pallas_call(
-        kernel,
-        out_shape=(jax.ShapeDtypeStruct(strong, F32), jax.ShapeDtypeStruct(weak, F32)),
-        in_specs=[smem] * 5 + [hbm] * 4 + [vmem, hbm] + [hbm] * 3 + [vmem, hbm],
-        out_specs=(hbm, hbm),
-        scratch_shapes=[
+    tiles = (POOL + 1, WIDE, WIDE)
+
+    def stay(x):
+        return pltpu.with_memory_space_constraint(x, pltpu.HBM)
+
+    kept = pl.pallas_call(
+        first_update,
+        out_shape=(
             pltpu.VMEM((SP, NB, WIDE, WIDE), BF16),
             pltpu.VMEM((WP, NB, SLIM, WIDE), BF16),
+            pltpu.VMEM(tiles, BF16),
+            pltpu.VMEM(strong, F32),
+            pltpu.VMEM(weak, F32),
+            pltpu.VMEM(strong, F32),
+            pltpu.VMEM(weak, F32),
+        ),
+        in_specs=[smem] * 5 + [hbm] * 4 + [vmem, hbm] + [hbm] * 3 + [vmem, hbm],
+        out_specs=(vmem,) * 7,
+        scratch_shapes=[
             pltpu.VMEM(strong, F32),
             pltpu.VMEM(strong, F32),
             pltpu.VMEM(strong, F32),
@@ -220,30 +291,42 @@
             pltpu.VMEM((WP, SLIM, WIDE), BF16),
             pltpu.VMEM(strong, F32),
             pltpu.VMEM(weak, F32),
-            pltpu.VMEM(strong, F32),
-            pltpu.VMEM(weak, F32),
-            pltpu.VMEM((POOL + 1, WIDE, WIDE), BF16),
-            pltpu.VMEM((POOL + 1, WIDE, WIDE), BF16),
+            pltpu.VMEM(tiles, BF16),
             pltpu.VMEM((len(COL_STEPS), CAP, WIDE, WIDE), BF16),
             pltpu.VMEM((len(COL_STEPS), CAP, WIDE, WIDE), BF16),
             pltpu.VMEM((len(ROW_STEPS), CAP, WIDE, WIDE), BF16),
             pltpu.VMEM((len(ROW_STEPS), CAP, WIDE, WIDE), BF16),
             pltpu.SemaphoreType.DMA((9,)),
-            pltpu.SemaphoreType.DMA((2,)),
             pltpu.SemaphoreType.DMA((2 * COLS,)),
             pltpu.SemaphoreType.DMA((2 * COLS,)),
             pltpu.SemaphoreType.DMA((2 * ROWS,)),
             pltpu.SemaphoreType.DMA((2 * ROWS,)),
         ],
         compiler_params=pltpu.CompilerParams(
-            collective_id=0, has_side_effects=True, vmem_limit_bytes=56 * 2**20
+            collective_id=0, has_side_effects=True, vmem_limit_bytes=32 * 2**20
         ),
-        name="amplitude_updates",
+        name="first_update",
     )(
-        strong_nb, strong_live, col_send, row_send, weak_nb,
-        strong_amp, strong_rhs, strong_left, strong_right, strong_energy, strong_intersection,
-        weak_amp, weak_rhs, weak_blocks, weak_energy, weak_intersection,
+        strong_nb, strong_live, col_send.T, row_send.T, weak_nb.T,
+        stay(strong_amp), stay(strong_rhs), stay(strong_left), stay(strong_right), strong_energy,
+        stay(strong_intersection), stay(weak_amp), stay(weak_rhs), stay(weak_blocks), weak_energy,
+        stay(weak_intersection),
     )
+    return pl.pallas_call(
+        second_update,
+        out_shape=(jax.ShapeDtypeStruct(strong, F32), jax.ShapeDtypeStruct(weak, F32)),
+        in_specs=[smem] * 3 + [vmem] * 7,
+        out_specs=(hbm, hbm),
+        scratch_shapes=[
+            pltpu.VMEM((SP + 1, WIDE, WIDE), F32),
+            pltpu.VMEM(strong, F32),
+            pltpu.VMEM(weak, F32),
+            pltpu.SemaphoreType.DMA((4,)),
+            pltpu.SemaphoreType.DMA((WP // WEAK_STEP,)),
+        ],
+        compiler_params=pltpu.CompilerParams(vmem_limit_bytes=24 * 2**20),
+        name="second_update",
+    )(strong_nb, strong_live, weak_nb.T, *kept)
 
 
 def solution(mesh):

time: 70.6 us -> 61.4 us (0.87); the launches traced: 70.3 us -> 61.9 us
  local copies, waits for them, and re-layouts: 8.67 us -> 0.01 us
    unnamed x5 -> x6, local copies, waits for them, and re-layouts: 8.67 us -> 0.01 us
    pallas_call x1 -> x2, Pallas kernels: 60.9 us -> 61.2 us  [the longest x1 43.3 us: on_device(): pl.pallas_call(first_update, out_shape=(pltpu.VMEM((SP, NB, WIDE, WIDE),...]
where the time goes in v2:
time: 61.4 us; the launch traced here: 61.9 us
  Pallas kernels  61.2 us (100%)
  between operations  0.69 us (1%)
    pallas_call x1, Pallas kernels, on_device(): pl.pallas_call(first_update, out_shape=(pltpu.VMEM((SP, NB, WIDE, WIDE),...  43.3 us
    pallas_call x1, Pallas kernels, on_device(): pl.pallas_call(second_update, out_shape=(jax.ShapeDtypeStruct(strong, F32...  17.9 us

profile of v2, /device:TPU:1, one launch (start us, length us, event | category | flops | bytes accessed | tf_op | source)
XLA Modules:
  0.0 61.9 jit_solution(4875153746745660394)
XLA Ops:
  0.6 0.0 copy-start
  0.6 0.0 copy-start.1
  0.7 0.0 copy-start.2
  0.7 43.3 %first_update.1 = (bf16[16,16,128,128]{3,2,1,0:T(8,128)(2,1)S(1)}, bf16[32,16,64,128]{3,2,1,0:T(8,128)(2,1)S(1)}, bf16[65,128,128]{2,1,0:T(8,128)(2,1)S(1)}, f32...) custom-call(s32[16,16]{1,0:T(8,128)} %s_nb.3, ...), custom_call_target="tpu_custom_call" | custom-call | tf_op jit(solution)/shard_map/first_update/pallas_call | solution.py:269
  44.0 0.0 copy-done
  44.0 0.0 copy-done.1
  44.0 0.0 copy-done.2
  44.0 17.9 %second_update.1 = (f32[16,128,128]{2,1,0:T(8,128)}, f32[32,64,64]{2,1,0:T(8,128)}) custom-call(s32[16,16]{1,0:T(8,128)S(1)} %copy-done, s32[16]{0:T(128)S(1)} %copy-done.2, s32[16,32]{1,0:T(8,128)S(1)} %bitcast.4, bf16[16,16,128,128]{3,2,1,0:T(8,128)(2,1)S(1)} %get-tuple-element.9.s_over, bf16[32,16,64,128]{3,2,1,0:T(8,128)(2,1)S(1)} %get-tuple-element.10.w_over, ...), custom_call_target="tpu_custom_call" | custom-call | tf_op jit(solution)/shard_map/second_update/pallas_call | solution.py:315
Async XLA Ops:
  0.6 43.4 %copy-start = (s32[16,16]{1,0:T(8,128)S(1)}, s32[16,16]{1,0:T(8,128)}, u32[]{:S(2)}) copy-start(s32[16,16]{1,0:T(8,128)} %s_nb.3) | copy-start | bytes 3076
  0.6 43.4 %copy-start.1 = (s32[32,16]{0,1:T(8,128)S(1)}, s32[32,16]{0,1:T(8,128)}, u32[]{:S(2)}) copy-start(s32[32,16]{0,1:T(8,128)} %param.31) | copy-start | bytes 6148
  0.7 43.4 %copy-start.2 = (s32[16]{0:T(128)S(1)}, s32[16]{0:T(128)}, u32[]{:S(2)}) copy-start(s32[16]{0:T(128)} %s_live.3) | copy-start | bytes 196

commit v3 on v2

--- a/solution.py
+++ b/solution.py
@@ -71,6 +71,12 @@
     def row_of(step):
         return lax.rem(y + step[0], DEPTH) * CORES + lax.rem(k + step[1], CORES)
 
+    barrier = pltpu.get_barrier_semaphore()
+    for step in COL_STEPS:
+        pl.semaphore_signal(barrier, inc=1, device_id=(r, col_of(step)), device_id_type=MESH)
+    for step in ROW_STEPS:
+        pl.semaphore_signal(barrier, inc=1, device_id=(row_of(step), c), device_id_type=MESH)
+
     loads = [
         pltpu.make_async_copy(source, place, load_sem.at[i])
         for i, (source, place) in enumerate(
@@ -82,12 +88,6 @@
     ]
     for load in loads:
         load.start()
-
-    barrier = pltpu.get_barrier_semaphore()
-    for step in COL_STEPS:
-        pl.semaphore_signal(barrier, inc=1, device_id=(r, col_of(step)), device_id_type=MESH)
-    for step in ROW_STEPS:
-        pl.semaphore_signal(barrier, inc=1, device_id=(row_of(step), c), device_id_type=MESH)
 
     def exchange(amp, pool, col_buf, row_buf, update, ready):
         base_col, base_row = update * COLS, update * ROWS
@@ -148,7 +148,7 @@
             total = coupling(s_over, p, pool, lambda n: jnp.where(n < s_live[p], s_nb[p, n], BLANK))
             new[p] = s_base[p] - total * s_inv[p]
 
-        looped(SP, 4, body)
+        looped(SP, 8, body)
 
     def weak_update(new, pool):
         def body(w):
@@ -186,72 +186,42 @@
         copy.wait()
 
 
-UNIT, UNITS, WEAK_STEP = 4, 8, 8
+STRONG_STEP, WEAK_STEP = 8, 16
 
 
 def second_update(
     s_nb, s_live, w_nb, s_over, w_over, pool, s_pre, w_pre, s_inv, w_inv,
-    s_out, w_out, s_sum, s_new, w_new, s_sem, w_sem,
+    s_out, w_out, s_new, w_new, s_sem, w_sem,
 ):
-    def parts(p):
-        return lax.div(s_live[p] + (UNIT - 1), UNIT)
-
-    total = parts(0)
-    for p in range(1, SP):
-        total = total + parts(p)
-
-    def strong_units(state):
-        p, j = state
-        for _ in range(UNITS):
-            real = p < SP
-            at = jnp.minimum(p, SP - 1)
-            live = jnp.where(real, s_live[at], 0)
-            mids = [
-                nn(s_over[at, j + t], pool[jnp.where(j + t < live, s_nb[at, j + t], BLANK)]).astype(BF16)
-                for t in range(UNIT)
-            ]
-            term = None
-            for t in range(0, UNIT, 2):
-                more = nt(
-                    jnp.concatenate([mids[t], mids[t + 1]], 1),
-                    jnp.concatenate([s_over[at, j + t], s_over[at, j + t + 1]], 1),
-                )
-                term = more if term is None else term + more
-            s_sum[p] = jnp.where(j == 0, 0.0, s_sum[p]) + term
-            last = j + UNIT >= live
-            p = jnp.where(last & real, p + 1, p)
-            j = jnp.where(last, 0, j + UNIT)
-        return p, j
+    def strong_copy(i):
+        rows = pl.ds(i * STRONG_STEP, STRONG_STEP)
+        return pltpu.make_async_copy(s_new.at[rows], s_out.at[rows], s_sem.at[i])
 
     def weak_copy(i):
         rows = pl.ds(i * WEAK_STEP, WEAK_STEP)
         return pltpu.make_async_copy(w_new.at[rows], w_out.at[rows], w_sem.at[i])
 
-    def both(i, state):
+    def strong(i, carry):
+        for u in range(STRONG_STEP):
+            p = i * STRONG_STEP + u
+            total = coupling(s_over, p, pool, lambda n: jnp.where(n < s_live[p], s_nb[p, n], BLANK))
+            s_new[p] = s_pre[p] - total * s_inv[p]
+        strong_copy(i).start()
+        return carry
+
+    def weak(i, carry):
         for u in range(WEAK_STEP):
             w = i * WEAK_STEP + u
             w_new[w] = w_pre[w] - coupling(w_over, w, pool, lambda n: w_nb[n, w]) * w_inv[w]
-        state = strong_units(state)
         weak_copy(i).start()
-        return state
-
-    steps = WP // WEAK_STEP
-    state = lax.fori_loop(0, steps, both, (jnp.int32(0), jnp.int32(0)))
-    rounds = lax.div(total + (UNITS - 1), UNITS)
-    lax.fori_loop(steps, rounds, lambda _, state: strong_units(state), state)
-
-    quarter = SP // 4
-    copies = []
-    for q in range(4):
-        for p in range(q * quarter, (q + 1) * quarter):
-            s_new[p] = s_pre[p] - s_sum[p] * s_inv[p]
-        rows = pl.ds(q * quarter, quarter)
-        copies.append(pltpu.make_async_copy(s_new.at[rows], s_out.at[rows], s_sem.at[q]))
-        copies[-1].start()
-    for i in range(steps):
+        return carry
+
+    lax.fori_loop(0, SP // STRONG_STEP, strong, 0)
+    lax.fori_loop(0, WP // WEAK_STEP, weak, 0)
+    for i in range(SP // STRONG_STEP):
+        strong_copy(i).wait()
+    for i in range(WP // WEAK_STEP):
         weak_copy(i).wait()
-    for copy in copies:
-        copy.wait()
 
 
 def on_device(
@@ -318,10 +288,9 @@
         in_specs=[smem] * 3 + [vmem] * 7,
         out_specs=(hbm, hbm),
         scratch_shapes=[
-            pltpu.VMEM((SP + 1, WIDE, WIDE), F32),
-            pltpu.VMEM(strong, F32),
-            pltpu.VMEM(weak, F32),
-            pltpu.SemaphoreType.DMA((4,)),
+            pltpu.VMEM(strong, F32),
+            pltpu.VMEM(weak, F32),
+            pltpu.SemaphoreType.DMA((SP // STRONG_STEP,)),
             pltpu.SemaphoreType.DMA((WP // WEAK_STEP,)),
         ],
         compiler_params=pltpu.CompilerParams(vmem_limit_bytes=24 * 2**20),

time: 61.4 us -> 57.4 us (0.935); the launches traced: 61.9 us -> 57.2 us
  Pallas kernels: 61.2 us -> 56.5 us
    pallas_call x1, Pallas kernels: 17.9 us -> 13.9 us  [on_device(): pl.pallas_call(second_update, out_shape=(jax.ShapeDtypeStruct(strong, F32...]
    pallas_call x1, Pallas kernels: 43.3 us -> 42.6 us  [on_device(): pl.pallas_call(first_update, out_shape=(pltpu.VMEM((SP, NB, WIDE, WIDE),...]
where the time goes in v3:
time: 57.4 us; the launch traced here: 57.2 us
  Pallas kernels  56.5 us (98%)
  between operations  0.69 us (1%)
    pallas_call x1, Pallas kernels, on_device(): pl.pallas_call(first_update, out_shape=(pltpu.VMEM((SP, NB, WIDE, WIDE),...  42.6 us
    pallas_call x1, Pallas kernels, on_device(): pl.pallas_call(second_update, out_shape=(jax.ShapeDtypeStruct(strong, F32...  13.9 us

profile of v3, /device:TPU:1, one launch (start us, length us, event | category | flops | bytes accessed | tf_op | source)
XLA Modules:
  0.0 57.2 jit_solution(12983613512405663823)
XLA Ops:
  0.6 0.0 copy-start
  0.6 0.0 copy-start.1
  0.7 0.0 copy-start.2
  0.7 42.6 %first_update.1 = (bf16[16,16,128,128]{3,2,1,0:T(8,128)(2,1)S(1)}, bf16[32,16,64,128]{3,2,1,0:T(8,128)(2,1)S(1)}, bf16[65,128,128]{2,1,0:T(8,128)(2,1)S(1)}, f32...) custom-call(s32[16,16]{1,0:T(8,128)} %s_nb.3, ...), custom_call_target="tpu_custom_call" | custom-call | tf_op jit(solution)/shard_map/first_update/pallas_call | solution.py:239
  43.3 0.0 copy-done
  43.3 0.0 copy-done.1
  43.3 0.0 copy-done.2
  43.3 13.9 %second_update.1 = (f32[16,128,128]{2,1,0:T(8,128)}, f32[32,64,64]{2,1,0:T(8,128)}) custom-call(s32[16,16]{1,0:T(8,128)S(1)} %copy-done, s32[16]{0:T(128)S(1)} %copy-done.2, s32[16,32]{1,0:T(8,128)S(1)} %bitcast.4, bf16[16,16,128,128]{3,2,1,0:T(8,128)(2,1)S(1)} %get-tuple-element.9.s_over, bf16[32,16,64,128]{3,2,1,0:T(8,128)(2,1)S(1)} %get-tuple-element.10.w_over, ...), custom_call_target="tpu_custom_call" | custom-call | tf_op jit(solution)/shard_map/second_update/pallas_call | solution.py:285
Async XLA Ops:
  0.6 42.7 %copy-start = (s32[16,16]{1,0:T(8,128)S(1)}, s32[16,16]{1,0:T(8,128)}, u32[]{:S(2)}) copy-start(s32[16,16]{1,0:T(8,128)} %s_nb.3) | copy-start | bytes 3076
  0.6 42.7 %copy-start.1 = (s32[32,16]{0,1:T(8,128)S(1)}, s32[32,16]{0,1:T(8,128)}, u32[]{:S(2)}) copy-start(s32[32,16]{0,1:T(8,128)} %param.31) | copy-start | bytes 6148
  0.7 42.7 %copy-start.2 = (s32[16]{0:T(128)S(1)}, s32[16]{0:T(128)}, u32[]{:S(2)}) copy-start(s32[16]{0:T(128)} %s_live.3) | copy-start | bytes 196

commit v4 on v3

--- a/solution.py
+++ b/solution.py
@@ -53,10 +53,11 @@
 
 
 def first_update(
-    s_nb, s_live, c_send, r_send, w_nb,
-    s_amp_h, s_rhs_h, s_left_h, s_right_h, s_en, s_over_h,
-    w_amp_h, w_rhs_h, w_blk_h, w_en, w_over_h,
-    s_over, w_over, pool_b, s_pre, w_pre, s_inv, w_inv,
+    s_nb_h, s_live_h, c_send_h, r_send_h, w_nb_h,
+    s_amp_h, s_rhs_h, s_left_h, s_right_h, s_en_h, s_over_h,
+    w_amp_h, w_rhs_h, w_blk_h, w_en_h, w_over_h,
+    s_over, w_over, pool_b, s_pre, w_pre, s_inv, w_inv, s_list, w_list,
+    s_nb, s_live, c_send, r_send, w_nb, s_en, w_en,
     s_amp, s_next, s_rhs, s_left, s_right, w_amp, w_next, w_rhs, w_blk, s_base, w_base,
     pool_a, col_a, col_b, row_a, row_b,
     load_sem, col_ss, col_rs, row_ss, row_rs,
@@ -81,8 +82,9 @@
         pltpu.make_async_copy(source, place, load_sem.at[i])
         for i, (source, place) in enumerate(
             (
-                (s_amp_h, s_amp), (s_left_h, s_left), (s_right_h, s_right), (s_rhs_h, s_rhs),
-                (w_amp_h, w_amp), (w_blk_h, w_blk), (w_rhs_h, w_rhs), (s_over_h, s_over), (w_over_h, w_over),
+                (c_send_h, c_send), (r_send_h, r_send), (s_amp_h, s_amp),
+                (s_en_h, s_en), (w_en_h, w_en), (s_nb_h, s_nb), (s_live_h, s_live), (w_nb_h, w_nb),
+                (s_left_h, s_left), (s_right_h, s_right), (s_rhs_h, s_rhs), (w_amp_h, w_amp), (w_blk_h, w_blk), (w_rhs_h, w_rhs), (s_over_h, s_over), (w_over_h, w_over),
             )
         )
     ]
@@ -145,7 +147,7 @@
 
     def strong_update(new, pool):
         def body(p):
-            total = coupling(s_over, p, pool, lambda n: jnp.where(n < s_live[p], s_nb[p, n], BLANK))
+            total = coupling(s_over, p, pool, lambda n: s_list[p, n])
             new[p] = s_base[p] - total * s_inv[p]
 
         looped(SP, 8, body)
@@ -157,8 +159,23 @@
 
         looped(WP, 8, body)
 
-    loads[0].wait()
+    for load in loads[:3]:
+        load.wait()
     copies = exchange(s_amp, pool_a, col_a, row_a, 0, lambda: pl.semaphore_wait(barrier, len(COL_STEPS) + len(ROW_STEPS)))
+
+    for load in loads[3:8]:
+        load.wait()
+
+    def strong_list(p):
+        for n in range(NB):
+            s_list[p, n] = jnp.where(n < s_live[p], s_nb[p, n], BLANK)
+
+    def weak_list(n):
+        for w in range(WP):
+            w_list[n, w] = w_nb[n, w]
+
+    looped(SP, 1, strong_list)
+    looped(NB, 1, weak_list)
 
     def strong_inverse(p):
         across = jnp.broadcast_to(s_en[pl.ds(p, 1), :], (WIDE, WIDE))
@@ -170,7 +187,7 @@
 
     looped(SP, 2, strong_inverse)
     looped(WP, 2, weak_inverse)
-    for load in loads[1:]:
+    for load in loads[8:]:
         load.wait()
     strong_base(s_amp, s_base)
     weak_base(w_amp, w_base)
@@ -190,7 +207,7 @@
 
 
 def second_update(
-    s_nb, s_live, w_nb, s_over, w_over, pool, s_pre, w_pre, s_inv, w_inv,
+    s_over, w_over, pool, s_pre, w_pre, s_inv, w_inv, s_list, w_list,
     s_out, w_out, s_new, w_new, s_sem, w_sem,
 ):
     def strong_copy(i):
@@ -204,7 +221,7 @@
     def strong(i, carry):
         for u in range(STRONG_STEP):
             p = i * STRONG_STEP + u
-            total = coupling(s_over, p, pool, lambda n: jnp.where(n < s_live[p], s_nb[p, n], BLANK))
+            total = coupling(s_over, p, pool, lambda n: s_list[p, n])
             s_new[p] = s_pre[p] - total * s_inv[p]
         strong_copy(i).start()
         return carry
@@ -212,7 +229,7 @@
     def weak(i, carry):
         for u in range(WEAK_STEP):
             w = i * WEAK_STEP + u
-            w_new[w] = w_pre[w] - coupling(w_over, w, pool, lambda n: w_nb[n, w]) * w_inv[w]
+            w_new[w] = w_pre[w] - coupling(w_over, w, pool, lambda n: w_list[n, w]) * w_inv[w]
         weak_copy(i).start()
         return carry
 
@@ -246,10 +263,19 @@
             pltpu.VMEM(weak, F32),
             pltpu.VMEM(strong, F32),
             pltpu.VMEM(weak, F32),
+            pltpu.SMEM((SP, NB), jnp.int32),
+            pltpu.SMEM((NB, WP), jnp.int32),
         ),
-        in_specs=[smem] * 5 + [hbm] * 4 + [vmem, hbm] + [hbm] * 3 + [vmem, hbm],
-        out_specs=(vmem,) * 7,
+        in_specs=[hbm] * 16,
+        out_specs=(vmem,) * 7 + (smem,) * 2,
         scratch_shapes=[
+            pltpu.SMEM((SP, NB), jnp.int32),
+            pltpu.SMEM((SP,), jnp.int32),
+            pltpu.SMEM((CAP, COLS), jnp.int32),
+            pltpu.SMEM((CAP, ROWS), jnp.int32),
+            pltpu.SMEM((NB, WP), jnp.int32),
+            pltpu.VMEM((SP, WIDE), F32),
+            pltpu.VMEM((WP, SLIM), F32),
             pltpu.VMEM(strong, F32),
             pltpu.VMEM(strong, F32),
             pltpu.VMEM(strong, F32),
@@ -266,7 +292,7 @@
             pltpu.VMEM((len(COL_STEPS), CAP, WIDE, WIDE), BF16),
             pltpu.VMEM((len(ROW_STEPS), CAP, WIDE, WIDE), BF16),
             pltpu.VMEM((len(ROW_STEPS), CAP, WIDE, WIDE), BF16),
-            pltpu.SemaphoreType.DMA((9,)),
+            pltpu.SemaphoreType.DMA((16,)),
             pltpu.SemaphoreType.DMA((2 * COLS,)),
             pltpu.SemaphoreType.DMA((2 * COLS,)),
             pltpu.SemaphoreType.DMA((2 * ROWS,)),
@@ -277,15 +303,16 @@
         ),
         name="first_update",
     )(
-        strong_nb, strong_live, col_send.T, row_send.T, weak_nb.T,
-        stay(strong_amp), stay(strong_rhs), stay(strong_left), stay(strong_right), strong_energy,
-        stay(strong_intersection), stay(weak_amp), stay(weak_rhs), stay(weak_blocks), weak_energy,
-        stay(weak_intersection),
+        *map(stay, (
+            strong_nb, strong_live, col_send.T, row_send.T, weak_nb.T,
+            strong_amp, strong_rhs, strong_left, strong_right, strong_energy, strong_intersection,
+            weak_amp, weak_rhs, weak_blocks, weak_energy, weak_intersection,
+        )),
     )
     return pl.pallas_call(
         second_update,
         out_shape=(jax.ShapeDtypeStruct(strong, F32), jax.ShapeDtypeStruct(weak, F32)),
-        in_specs=[smem] * 3 + [vmem] * 7,
+        in_specs=[vmem] * 7 + [smem] * 2,
         out_specs=(hbm, hbm),
         scratch_shapes=[
             pltpu.VMEM(strong, F32),
@@ -295,7 +322,7 @@
         ],
         compiler_params=pltpu.CompilerParams(vmem_limit_bytes=24 * 2**20),
         name="second_update",
-    )(strong_nb, strong_live, weak_nb.T, *kept)
+    )(*kept)
 
 
 def solution(mesh):

time: 57.4 us -> 55.6 us (0.969)
  Pallas kernels: 56.5 us -> 54.8 us
    pallas_call x1, Pallas kernels: 42.6 us -> 41.7 us  [on_device(): pl.pallas_call(first_update, out_shape=(pltpu.VMEM((SP, NB, WIDE, WIDE),...]
    pallas_call x1, Pallas kernels: 13.9 us -> 13.1 us  [on_device(): pl.pallas_call(second_update, out_shape=(jax.ShapeDtypeStruct(strong, F32...]
where the time goes in v4:
time: 55.6 us; the launch traced here: 55.5 us
  Pallas kernels  54.8 us (99%)
  between operations  0.64 us (1%)
    pallas_call x1, Pallas kernels, on_device(): pl.pallas_call(first_update, out_shape=(pltpu.VMEM((SP, NB, WIDE, WIDE),...  41.7 us
    pallas_call x1, Pallas kernels, on_device(): pl.pallas_call(second_update, out_shape=(jax.ShapeDtypeStruct(strong, F32...  13.1 us

profile of v4, /device:TPU:1, one launch (start us, length us, event | category | flops | bytes accessed | tf_op | source)
XLA Modules:
  0.0 55.5 jit_solution(153755288714192587)
XLA Ops:
  0.6 41.7 %first_update.1 = (bf16[16,16,128,128]{3,2,1,0:T(8,128)(2,1)S(1)}, bf16[32,16,64,128]{3,2,1,0:T(8,128)(2,1)S(1)}, bf16[65,128,128]{2,1,0:T(8,128)(2,1)S(1)}, f32...) custom-call(s32[16,16]{1,0:T(8,128)} %s_nb_h.1, ...), custom_call_target="tpu_custom_call" | custom-call | tf_op jit(solution)/shard_map/first_update/pallas_call | solution.py:256
  42.4 13.1 %second_update.1 = (f32[16,128,128]{2,1,0:T(8,128)}, f32[32,64,64]{2,1,0:T(8,128)}) custom-call(bf16[16,16,128,128]{3,2,1,0:T(8,128)(2,1)S(1)} %get-tuple-element.11.s_over, bf16[32,16,64,128]{3,2,1,0:T(8,128)(2,1)S(1)} %get-tuple-element.12.w_over, bf16[65,128,128]{2,1,0:T(8,128)(2,1)S(1)} %get-tuple-element.13.pool, ...), custom_call_target="tpu_custom_call" | custom-call | tf_op jit(solution)/shard_map/second_update/pallas_call | solution.py:312

commit v5 on v4

--- a/solution.py
+++ b/solution.py
@@ -203,7 +203,7 @@
         copy.wait()
 
 
-STRONG_STEP, WEAK_STEP = 8, 16
+STRONG_STEP, WEAK_STEP = 16, 32
 
 
 def second_update(

time: 55.6 us -> 55.1 us (level)
  Pallas kernels: 54.8 us -> 54.2 us
    pallas_call x1, Pallas kernels: 13.1 us -> 12.4 us  [on_device(): pl.pallas_call(second_update, out_shape=(jax.ShapeDtypeStruct(strong, F32...]
where the time goes in v5:
time: 55.1 us; the launch traced here: 55 us
  Pallas kernels  54.2 us (98%)
  between operations  0.81 us (1%)
    pallas_call x1, Pallas kernels, on_device(): pl.pallas_call(first_update, out_shape=(pltpu.VMEM((SP, NB, WIDE, WIDE),...  41.7 us
    pallas_call x1, Pallas kernels, on_device(): pl.pallas_call(second_update, out_shape=(jax.ShapeDtypeStruct(strong, F32...  12.4 us

profile of v5, /device:TPU:1, one launch (start us, length us, event | category | flops | bytes accessed | tf_op | source)
XLA Modules:
  0.0 55.0 jit_solution(484646334241947224)
XLA Ops:
  0.6 41.7 %first_update.1 = (bf16[16,16,128,128]{3,2,1,0:T(8,128)(2,1)S(1)}, bf16[32,16,64,128]{3,2,1,0:T(8,128)(2,1)S(1)}, bf16[65,128,128]{2,1,0:T(8,128)(2,1)S(1)}, f32...) custom-call(s32[16,16]{1,0:T(8,128)} %s_nb_h.1, ...), custom_call_target="tpu_custom_call" | custom-call | tf_op jit(solution)/shard_map/first_update/pallas_call | solution.py:256
  42.4 12.4 %second_update.1 = (f32[16,128,128]{2,1,0:T(8,128)}, f32[32,64,64]{2,1,0:T(8,128)}) custom-call(bf16[16,16,128,128]{3,2,1,0:T(8,128)(2,1)S(1)} %get-tuple-element.11.s_over, bf16[32,16,64,128]{3,2,1,0:T(8,128)(2,1)S(1)} %get-tuple-element.12.w_over, bf16[65,128,128]{2,1,0:T(8,128)(2,1)S(1)} %get-tuple-element.13.pool, ...), custom_call_target="tpu_custom_call" | custom-call | tf_op jit(solution)/shard_map/second_update/pallas_call | solution.py:312
